TPU v7x, 128 devices: a whole 4x4x4 slice. The times are simulated.
128 devices in a mesh: emb: 8 (over x, core), seq: 16 (over z, y).
Axes of the slice: x: 4, y: 4, z: 4, core: 2. Of those that a mesh axis runs over, the one named last changes fastest.
Arguments:
- token_rows: int32 [8, 8192], P('emb', 'seq'), may hold values from 0 to 4607, as said below
- segment_ids: int32 [8, 8192], P('emb', 'seq'), may hold values from 0 to 3, never falling along the last dimension, each value on 1 to 4096 neighbouring positions
- requests: int32 [128, 128, 4], P(('emb', 'seq')), may hold values from 0 to 8191, as said below
- hot_table: bfloat16 [4096, 512], replicated, may hold values from -6 to 6
- cold_table: bfloat16 [1048576, 512], P(('emb', 'seq')), may hold values from -6 to 6
- input_weight: bfloat16 [512, 2048], replicated, may hold values from -0.75 to 0.75
- output_weight: bfloat16 [512, 512], replicated, may hold values from -0.25 to 0.25
- up_weight: bfloat16 [512, 2048], replicated, may hold values from -0.25 to 0.25
- down_weight: bfloat16 [2048, 512], replicated, may hold values from -0.125 to 0.125
Outputs:
- layer_output: bfloat16 [8, 8192, 512], P('emb', 'seq')
Inputs may be any that keep to these rules, and one draw needn't show every extreme that they name: `token_rows`: A value below 4096 names that row of hot_table. A value 4096 + o * 4 + k names slot k of the holding device's requests to owner o, and that slot is always a live one. Exactly 256 positions of each device name request slots. For each requesting device and owner the live requests fill slots 0 to c - 1, with c from 1 to 4; dead slots hold 0. Some owners, the same ones for all requesters, get all 4 slots live from every device, and every draw has at least one such owner. `segment_ids`: segment numbers never fall along a sequence.
All inputs are finite; a program needn't handle non-finite values.
Results may differ from a plain program's by a relative error of at most 0.0087.
Values may be sent and summed in bfloat16 or wider, within the bound.
A program may use at most 128 MiB of HBM per device.

v0:
```python
import math
import jax
import jax.numpy as jnp
from jax import lax
from jax.sharding import PartitionSpec as P

H = 16
epsilon = 1e-06


def in_order(pieces, dim):
    shape = list(pieces.shape[1:])
    shape[dim] *= pieces.shape[0]
    return jnp.moveaxis(pieces, 0, dim).reshape(shape)


def copy_for_each(value, axis):
    devices = lax.axis_size(axis)
    return lax.all_to_all(
        jnp.broadcast_to(value[None], (devices, *value.shape)), axis, 0, 0, tiled=True
    )


def collect(value, axis, dim):
    return in_order(copy_for_each(value, axis), dim)


def normalize(values):
    widened = values.astype(jnp.float32)
    return widened * lax.rsqrt(jnp.mean(widened * widened, axis=-1, keepdims=True) + epsilon)


def attend(queries, key_rows, value_rows, segments):
    length, groups, head_width = queries.shape
    block_rows = math.gcd(length, 2048)
    blocks = length // block_rows
    score_scale = 1.0 / math.sqrt(head_width)
    query_blocks = queries.reshape(blocks, block_rows, groups, head_width)
    key_blocks = key_rows.reshape(blocks, block_rows, groups, head_width)
    value_blocks = value_rows.reshape(blocks, block_rows, groups, head_width)
    segment_blocks = segments.reshape(blocks, block_rows)
    offsets = jnp.arange(block_rows, dtype=jnp.int32)

    def one_block(inputs):
        query_block, query_segments, position = inputs
        query_places = position * block_rows + offsets

        def add_keys(key_step, running):
            key_block = lax.dynamic_index_in_dim(key_blocks, key_step, 0, keepdims=False)
            value_block = lax.dynamic_index_in_dim(value_blocks, key_step, 0, keepdims=False)
            key_segments = lax.dynamic_index_in_dim(segment_blocks, key_step, 0, keepdims=False)
            key_places = key_step * block_rows + offsets
            scores = (
                jnp.einsum(
                    "qgc,kgc->gqk", query_block, key_block, preferred_element_type=jnp.float32
                )
                * score_scale
            )
            allowed = (key_places[None, :] <= query_places[:, None]) & (
                query_segments[:, None] == key_segments[None, :]
            )
            weights = jnp.where(allowed[None], jax.nn.silu(scores), 0.0).astype(jnp.bfloat16)
            return running + jnp.einsum(
                "gqk,kgc->qgc", weights, value_block, preferred_element_type=jnp.float32
            )

        running = lax.fori_loop(
            0, position + 1, add_keys, jnp.zeros((block_rows, groups, head_width), jnp.float32)
        )
        return running.astype(jnp.bfloat16)

    attended = lax.map(
        one_block, (query_blocks, segment_blocks, jnp.arange(blocks, dtype=jnp.int32))
    )
    return attended.reshape(length, groups, head_width)


def local(
    token_rows,
    segment_ids,
    requests,
    hot_table,
    cold_table,
    input_weight,
    output_weight,
    up_weight,
    down_weight,
):
    emb_devices = lax.axis_size("emb")
    seq_devices = lax.axis_size("seq")
    all_devices = emb_devices * seq_devices
    capacity = requests.shape[2]
    hot_count = hot_table.shape[0]
    model_width = hot_table.shape[1]
    tokens_here = token_rows.shape[1]
    head_groups = H // seq_devices
    head_width = model_width // H
    requested = requests[0]
    fetched = lax.all_to_all(
        cold_table[
            lax.all_to_all(requested, ("emb", "seq"), split_axis=0, concat_axis=0, tiled=True)
        ],
        ("emb", "seq"),
        split_axis=0,
        concat_axis=0,
        tiled=True,
    )
    fetched = fetched.reshape(all_devices * capacity, model_width)
    item_ids = token_rows[0]
    is_hot = item_ids < hot_count
    hot_rows = hot_table[jnp.where(is_hot, item_ids, 0)]
    cold_rows = fetched[jnp.where(is_hot, 0, item_ids - hot_count)]
    embedded = jnp.where(is_hot[:, None], hot_rows, cold_rows)
    normed_input = normalize(embedded).astype(jnp.bfloat16)
    grouped_weight = input_weight.reshape(model_width, seq_devices, head_groups, 4, head_width)
    segments = collect(segment_ids, "seq", 1)[0]
    gate_rounded = jnp.einsum(
        "td,dgec->gtec",
        normed_input,
        grouped_weight[:, :, :, 0, :],
        preferred_element_type=jnp.float32,
    ).astype(jnp.bfloat16)
    gate_units = jax.nn.silu(lax.optimization_barrier(gate_rounded).astype(jnp.float32))
    own_group = lax.axis_index("seq")
    own_weight = lax.dynamic_index_in_dim(grouped_weight, own_group, 1, keepdims=False)[
        :, :, 1:, :
    ].reshape(model_width, head_groups * 3 * head_width)
    gathered = jnp.dot(
        lax.all_gather(normed_input, "seq", axis=0, tiled=True),
        own_weight,
        preferred_element_type=jnp.float32,
    ).astype(jnp.bfloat16)
    head_rows = gathered.reshape(tokens_here * seq_devices, head_groups, 3, head_width)
    attended = attend(head_rows[:, :, 1], head_rows[:, :, 2], head_rows[:, :, 0], segments)
    returned = lax.all_to_all(
        attended.reshape(seq_devices, tokens_here * head_groups * head_width),
        "seq",
        split_axis=0,
        concat_axis=0,
        tiled=True,
    )
    returned = returned.reshape(seq_devices, tokens_here, head_groups, head_width).astype(
        jnp.float32
    )
    mean_square = jnp.mean(returned * returned, axis=(0, 2, 3))
    normed_heads = (
        returned * lax.rsqrt(mean_square + epsilon)[None, :, None, None] * gate_units
    ).astype(jnp.bfloat16)
    hidden = embedded.astype(jnp.float32) + jnp.einsum(
        "gtc,gcd->td",
        normed_heads.reshape(seq_devices, tokens_here, head_groups * head_width),
        output_weight.reshape(seq_devices, head_groups * head_width, model_width),
        preferred_element_type=jnp.float32,
    )
    normed_hidden = normalize(hidden).astype(jnp.bfloat16)
    activated = jax.nn.silu(
        jnp.dot(normed_hidden, up_weight, preferred_element_type=jnp.float32)
    ).astype(jnp.bfloat16)
    layer_output = (
        hidden + jnp.dot(activated, down_weight, preferred_element_type=jnp.float32)
    ).astype(jnp.bfloat16)
    return layer_output[None]


def solution(mesh):
    placed = (
        P("emb", "seq"),
        P("emb", "seq"),
        P(("emb", "seq"), None, None),
        P(),
        P(("emb", "seq"), None),
        P(),
        P(),
        P(),
        P(),
    )
    return jax.shard_map(
        local, mesh=mesh, in_specs=placed, out_specs=P("emb", "seq", None), check_vma=False
    )
```

profile of v0, /device:TPU:0, one launch (start us, length us, event | category | flops | bytes accessed | tf_op | source)
XLA Modules:
  0.0 304.7 jit_solution(13476258196587185154)
XLA Ops:
  7.5 20.5 %all_to_all.32 = s32[128,1,4]{2,1,0:T(1,128)S(1)} all-to-all(s32[128,1,4]{2,1,0:T(1,128)S(1)} %bitcast.141), channel_id=1, replica_groups=mesh['emb'=8,'seq'=16] {'emb','seq'}, dimensions={0} | all-to-all | bytes 4096 | tf_op jit(solution)/shard_map/all_to_all | solution.py:101
  28.1 6.4 %gather_fusion.1 = bf16[512,512]{1,0:T(8,128)(2,1)S(1)} fusion(bf16[8192,512]{1,0:T(8,128)(2,1)} %param.17, s32[1024]{0:T(1024)S(1)} %pad_clamp_fusion.1), kind=kCustom, calls=%fused_computation.1 | custom fusion | bytes 1050624 | tf_op jit(solution)/shard_map/gather | solution.py:100
  35.5 5.7 %all-to-all-start.1 = ((bf16[128,4,512]{2,1,0:T(4,128)(2,1)}), bf16[128,4,512]{2,1,0:T(4,128)(2,1)}, u32[]{:S(2)}, u32[]{:S(2)}) async-start(bf16[128,4,512]{2,1,0:T(4,128)(2,1)} %reshape.217), calls=%async_computation.1 | async-start | bytes 1048576 | tf_op jit(solution)/shard_map/all_to_all | solution.py:99
  41.3 4.7 %gather_fusion = bf16[512,512]{1,0:T(8,128)(2,1)S(1)} fusion(bf16[4096,512]{1,0:T(8,128)(2,1)} %param.16, s32[1024]{0:T(1024)S(1)} %pad_clamp_fusion.2), kind=kCustom, calls=%fused_computation | custom fusion | bytes 1050624 | tf_op jit(solution)/shard_map/gather | solution.py:111
  46.3 8.1 %all-to-all-done.1 = bf16[128,4,512]{2,1,0:T(4,128)(2,1)} async-done(((bf16[128,4,512]{2,1,0:T(4,128)(2,1)}), bf16[128,4,512]{2,1,0:T(4,128)(2,1)}, u32[]{:S(2)}, u32[]{:S(2)}) %all-to-all-start.1) | async-done | bytes 524320 | tf_op jit(solution)/shard_map/all_to_all | solution.py:99
  54.4 1.2 reshape.200
  55.6 2.6 gather_fusion.2
  58.2 1.3 copy.45
  62.1 3.7 %all-to-all-start.2 = ((s32[16,1,512]{2,1,0:T(1,128)}), s32[16,1,512]{2,1,0:T(1,128)S(1)}, u32[]{:S(2)}, u32[]{:S(2)}) async-start(s32[16,1,512]{2,1,0:T(1,128)} %broadcast_in_dim.52), calls=%async_computation.2 | async-start | bytes 65536 | tf_op jit(solution)/shard_map/all_to_all | solution.py:19
  65.7 4.0 %copy.46 = bf16[512,2048]{0,1:T(8,128)(2,1)} copy(bf16[512,2048]{1,0:T(8,128)(2,1)} %param.18) | data formatting | bytes 4194304 | tf_op args[5]
  70.6 1.9 slice.30
  73.2 61.5 %all-gather.2.cloned.1.call-done = bf16[8192,512]{0,1:T(8,128)(2,1)} async-done(((bf16[512,512]{0,1:T(8,128)(2,1)}), bf16[8192,512]{0,1:T(8,128)(2,1)}) %all-gather.2.cloned.1.call-update) | async-done | bytes 8388624 | tf_op jit(solution)/shard_map/all_gather | solution.py:129
  134.7 4.8 %convolution_convert_fusion = bf16[8192,96]{0,1:T(8,128)(2,1)S(1)} fusion(bf16[512,96]{0,1:T(8,128)(2,1)S(1)} %bitcast.139, bf16[8192,512]{0,1:T(8,128)(2,1)} %all-gather.2.cloned.1.call-done), kind=kOutput, calls=%fused_computation.29 | convolution fusion | flops 806092800 | bytes 10059776 | tf_op jit(solution)/shard_map/dot_general | solution.py:128
  139.6 1.1 fusion.43
  140.7 1.2 reshape_squeeze.9
  141.9 1.3 copy.47
  143.2 2.2 reshape_squeeze.10
  145.4 2.1 copy.48
  147.5 2.2 reshape_squeeze.11
  149.8 2.1 copy.49
  151.9 93.7 %while.25 = (s32[]{:T(128)}, bf16[4,2048,1,32]{1,3,2,0:T(8,128)(2,1)}, s32[4]{0:T(128)S(1)}, bf16[4,2048,1,32]{1,3,2,0:T(8,128)(2,1)S(1)}, s32[4,2048]{1,0:T(4,1...) while((s32[]{:T(128)}, ...), condition=%wide.region_4.5_spmd.clone.clone, body=%wide.region_1.4_spmd.clone.clone.sunk | while | flops 578949120 | bytes 1934864 | solution.py:72
  153.9 8.3 %while.26 = (s32[]{:T(128)}, f32[2048,1,32]{0,2,1:T(8,128)S(1)}, s32[]{:T(128)}, bf16[4,2048,1,32]{1,3,2,0:T(8,128)(2,1)}, s32[2048]{0:T(1024)S(1)}, /*index=5*/...) while((s32[]{:T(128)}, f32[2048,1,32]{0,2,1:T(8,128)S(1)}, ...), condition=%wide.region_3.3_spmd, body=%wide.region_2.2_spmd.sunk | while | flops 578881536 | bytes 984259 | solution.py:67
  154.0 8.2 %fusion.59 = f32[2048,1,32]{0,2,1:T(8,128)S(1)} fusion(f32[2048,1,32]{0,2,1:T(8,128)S(1)} %get-tuple-element.351, s32[2048]{0:T(1024)S(1)} %get-tuple-element.370, s32[2048]{0:T(1024)S(1)} %get-tuple-element.369, s32[2048]{0:T(1024)S(1)} %bitcast.134, s32[2048]{0:T(1024)S(1)} %broadcast_add_fusion.2, ...), kind=kOutput, calls=%fused_computation.13.clone.1 | convolution fusion | flops 578879488 | bytes 951296 | tf_op jit(solution)/shard_map/while/body/eval_jaxpr/while/body/gqk,kgc->qgc/dot_general | solution.py:63
  164.9 16.6 %while.26 = (s32[]{:T(128)}, f32[2048,1,32]{0,2,1:T(8,128)S(1)}, s32[]{:T(128)}, bf16[4,2048,1,32]{1,3,2,0:T(8,128)(2,1)}, s32[2048]{0:T(1024)S(1)}, /*index=5*/...) while((s32[]{:T(128)}, f32[2048,1,32]{0,2,1:T(8,128)S(1)}, ...), condition=%wide.region_3.3_spmd, body=%wide.region_2.2_spmd.sunk | while | flops 578881536 | bytes 984259 | solution.py:67
  164.9 8.3 %fusion.59 = f32[2048,1,32]{0,2,1:T(8,128)S(1)} fusion(f32[2048,1,32]{0,2,1:T(8,128)S(1)} %get-tuple-element.351, s32[2048]{0:T(1024)S(1)} %get-tuple-element.370, s32[2048]{0:T(1024)S(1)} %get-tuple-element.369, s32[2048]{0:T(1024)S(1)} %bitcast.134, s32[2048]{0:T(1024)S(1)} %broadcast_add_fusion.2, ...), kind=kOutput, calls=%fused_computation.13.clone.1 | convolution fusion | flops 578879488 | bytes 951296 | tf_op jit(solution)/shard_map/while/body/eval_jaxpr/while/body/gqk,kgc->qgc/dot_general | solution.py:63
  173.3 8.2 %fusion.59 = f32[2048,1,32]{0,2,1:T(8,128)S(1)} fusion(f32[2048,1,32]{0,2,1:T(8,128)S(1)} %get-tuple-element.351, s32[2048]{0:T(1024)S(1)} %get-tuple-element.370, s32[2048]{0:T(1024)S(1)} %get-tuple-element.369, s32[2048]{0:T(1024)S(1)} %bitcast.134, s32[2048]{0:T(1024)S(1)} %broadcast_add_fusion.2, ...), kind=kOutput, calls=%fused_computation.13.clone.1 | convolution fusion | flops 578879488 | bytes 951296 | tf_op jit(solution)/shard_map/while/body/eval_jaxpr/while/body/gqk,kgc->qgc/dot_general | solution.py:63
  184.2 24.9 %while.26 = (s32[]{:T(128)}, f32[2048,1,32]{0,2,1:T(8,128)S(1)}, s32[]{:T(128)}, bf16[4,2048,1,32]{1,3,2,0:T(8,128)(2,1)}, s32[2048]{0:T(1024)S(1)}, /*index=5*/...) while((s32[]{:T(128)}, f32[2048,1,32]{0,2,1:T(8,128)S(1)}, ...), condition=%wide.region_3.3_spmd, body=%wide.region_2.2_spmd.sunk | while | flops 578881536 | bytes 984259 | solution.py:67
  184.2 8.2 %fusion.59 = f32[2048,1,32]{0,2,1:T(8,128)S(1)} fusion(f32[2048,1,32]{0,2,1:T(8,128)S(1)} %get-tuple-element.351, s32[2048]{0:T(1024)S(1)} %get-tuple-element.370, s32[2048]{0:T(1024)S(1)} %get-tuple-element.369, s32[2048]{0:T(1024)S(1)} %bitcast.134, s32[2048]{0:T(1024)S(1)} %broadcast_add_fusion.2, ...), kind=kOutput, calls=%fused_computation.13.clone.1 | convolution fusion | flops 578879488 | bytes 951296 | tf_op jit(solution)/shard_map/while/body/eval_jaxpr/while/body/gqk,kgc->qgc/dot_general | solution.py:63
  192.5 8.2 %fusion.59 = f32[2048,1,32]{0,2,1:T(8,128)S(1)} fusion(f32[2048,1,32]{0,2,1:T(8,128)S(1)} %get-tuple-element.351, s32[2048]{0:T(1024)S(1)} %get-tuple-element.370, s32[2048]{0:T(1024)S(1)} %get-tuple-element.369, s32[2048]{0:T(1024)S(1)} %bitcast.134, s32[2048]{0:T(1024)S(1)} %broadcast_add_fusion.2, ...), kind=kOutput, calls=%fused_computation.13.clone.1 | convolution fusion | flops 578879488 | bytes 951296 | tf_op jit(solution)/shard_map/while/body/eval_jaxpr/while/body/gqk,kgc->qgc/dot_general | solution.py:63
  200.8 8.2 %fusion.59 = f32[2048,1,32]{0,2,1:T(8,128)S(1)} fusion(f32[2048,1,32]{0,2,1:T(8,128)S(1)} %get-tuple-element.351, s32[2048]{0:T(1024)S(1)} %get-tuple-element.370, s32[2048]{0:T(1024)S(1)} %get-tuple-element.369, s32[2048]{0:T(1024)S(1)} %bitcast.134, s32[2048]{0:T(1024)S(1)} %broadcast_add_fusion.2, ...), kind=kOutput, calls=%fused_computation.13.clone.1 | convolution fusion | flops 578879488 | bytes 951296 | tf_op jit(solution)/shard_map/while/body/eval_jaxpr/while/body/gqk,kgc->qgc/dot_general | solution.py:63
  211.7 33.2 %while.26 = (s32[]{:T(128)}, f32[2048,1,32]{0,2,1:T(8,128)S(1)}, s32[]{:T(128)}, bf16[4,2048,1,32]{1,3,2,0:T(8,128)(2,1)}, s32[2048]{0:T(1024)S(1)}, /*index=5*/...) while((s32[]{:T(128)}, f32[2048,1,32]{0,2,1:T(8,128)S(1)}, ...), condition=%wide.region_3.3_spmd, body=%wide.region_2.2_spmd.sunk | while | flops 578881536 | bytes 984259 | solution.py:67
  211.8 8.2 %fusion.59 = f32[2048,1,32]{0,2,1:T(8,128)S(1)} fusion(f32[2048,1,32]{0,2,1:T(8,128)S(1)} %get-tuple-element.351, s32[2048]{0:T(1024)S(1)} %get-tuple-element.370, s32[2048]{0:T(1024)S(1)} %get-tuple-element.369, s32[2048]{0:T(1024)S(1)} %bitcast.134, s32[2048]{0:T(1024)S(1)} %broadcast_add_fusion.2, ...), kind=kOutput, calls=%fused_computation.13.clone.1 | convolution fusion | flops 578879488 | bytes 951296 | tf_op jit(solution)/shard_map/while/body/eval_jaxpr/while/body/gqk,kgc->qgc/dot_general | solution.py:63
  220.1 8.2 %fusion.59 = f32[2048,1,32]{0,2,1:T(8,128)S(1)} fusion(f32[2048,1,32]{0,2,1:T(8,128)S(1)} %get-tuple-element.351, s32[2048]{0:T(1024)S(1)} %get-tuple-element.370, s32[2048]{0:T(1024)S(1)} %get-tuple-element.369, s32[2048]{0:T(1024)S(1)} %bitcast.134, s32[2048]{0:T(1024)S(1)} %broadcast_add_fusion.2, ...), kind=kOutput, calls=%fused_computation.13.clone.1 | convolution fusion | flops 578879488 | bytes 951296 | tf_op jit(solution)/shard_map/while/body/eval_jaxpr/while/body/gqk,kgc->qgc/dot_general | solution.py:63
  228.4 8.2 %fusion.59 = f32[2048,1,32]{0,2,1:T(8,128)S(1)} fusion(f32[2048,1,32]{0,2,1:T(8,128)S(1)} %get-tuple-element.351, s32[2048]{0:T(1024)S(1)} %get-tuple-element.370, s32[2048]{0:T(1024)S(1)} %get-tuple-element.369, s32[2048]{0:T(1024)S(1)} %bitcast.134, s32[2048]{0:T(1024)S(1)} %broadcast_add_fusion.2, ...), kind=kOutput, calls=%fused_computation.13.clone.1 | convolution fusion | flops 578879488 | bytes 951296 | tf_op jit(solution)/shard_map/while/body/eval_jaxpr/while/body/gqk,kgc->qgc/dot_general | solution.py:63
  236.7 8.2 %fusion.59 = f32[2048,1,32]{0,2,1:T(8,128)S(1)} fusion(f32[2048,1,32]{0,2,1:T(8,128)S(1)} %get-tuple-element.351, s32[2048]{0:T(1024)S(1)} %get-tuple-element.370, s32[2048]{0:T(1024)S(1)} %get-tuple-element.369, s32[2048]{0:T(1024)S(1)} %bitcast.134, s32[2048]{0:T(1024)S(1)} %broadcast_add_fusion.2, ...), kind=kOutput, calls=%fused_computation.13.clone.1 | convolution fusion | flops 578879488 | bytes 951296 | tf_op jit(solution)/shard_map/while/body/eval_jaxpr/while/body/gqk,kgc->qgc/dot_general | solution.py:63
  245.6 2.7 copy.50
  248.4 5.4 %all_to_all.27 = bf16[16,1,16384]{2,1,0:T(2,128)(2,1)} reshape(bf16[4,2048,1,32]{3,1,0,2:T(8,128)(2,1)} %copy.50) | data formatting | bytes 1048576 | tf_op jit(solution)/shard_map/all_to_all | solution.py:135
  254.4 5.0 %reduce.9 = bf16[16,16384]{1,0:T(8,128)(2,1)S(1)} reduce(bf16[16,1,16384]{2,1,0:T(2,128)(2,1)} %all_to_all.27, bf16[]{:T(256)} %broadcast.198), dimensions={1}, to_apply=%all_to_all.27.reduce_sub_computation | reduce | bytes 1048578 | tf_op jit(solution)/shard_map/all_to_all | solution.py:135
  259.4 1.2 reshape.239
  260.5 4.9 %all-to-all-start.3 = ((bf16[16,2,8192]{2,1,0:T(2,128)(2,1)}), bf16[16,2,8192]{2,1,0:T(2,128)(2,1)S(1)}, u32[]{:S(2)}, u32[]{:S(2)}) async-start(bf16[16,2,8192]{2,1,0:T(2,128)(2,1)} %reshape.239), calls=%async_computation.3 | async-start | bytes 1048576 | tf_op jit(solution)/shard_map/all_to_all | solution.py:135
  265.5 1.5 fusion.44
  267.9 7.9 %all-to-all-done.3 = bf16[16,2,8192]{2,1,0:T(2,128)(2,1)S(1)} async-done(((bf16[16,2,8192]{2,1,0:T(2,128)(2,1)}), bf16[16,2,8192]{2,1,0:T(2,128)(2,1)S(1)}, u32[]{:S(2)}, u32[]{:S(2)}) %all-to-all-start.3) | async-done | bytes 524320 | tf_op jit(solution)/shard_map/all_to_all | solution.py:135
  275.7 1.8 reshape.240
  277.5 4.7 %fusion.33 = (f32[16384]{0:T(1024)S(1)}, f32[16,16384]{1,0:T(8,128)S(1)}) fusion(bf16[16,1,16384]{2,1,0:T(2,128)(2,1)} %reshape.240), kind=kLoop, calls=%fused_computation.49 | loop fusion | flops 770048 | bytes 1638400 | tf_op jit(solution)/shard_map/reduce_sum | solution.py:145
  282.2 2.7 reshape.207
  284.9 3.7 %copy.52 = f32[16,512,1,32]{1,3,0,2:T(8,128)} copy(f32[16,512,1,32]{3,1,0,2:T(8,128)} %reshape.207) | data formatting | bytes 2097152 | tf_op jit(solution)/shard_map/convert_element_type | solution.py:142
  288.9 3.0 multiply_reduce_fusion
  291.9 5.0 %fusion.26 = bf16[1,512,512]{1,2,0:T(8,128)(2,1)S(1)} fusion(f32[512,512]{0,1:T(8,128)} %get-tuple-element.207, bf16[2048,512]{1,0:T(8,128)(2,1)S(1)} %copy-done, bf16[512,2048]{1,0:T(8,128)(2,1)} %param.20, f32[512]{0:T(512)S(1)} %add_rsqrt_fusion), kind=kOutput, calls=%fused_computation.40 | convolution fusion | flops 2153775104 | bytes 5769216 | tf_op jit(solution)/shard_map/dot_general | solution.py:160
  (92 shorter events, 14.7 us)
Async XLA Ops:
  6.5 285.4 %copy-start = (bf16[2048,512]{1,0:T(8,128)(2,1)S(1)}, bf16[2048,512]{1,0:T(8,128)(2,1)}, u32[]{:S(2)}) copy-start(bf16[2048,512]{1,0:T(8,128)(2,1)} %param.21) | copy-start | bytes 6291460
  6.5 34.7 %copy-start.5 = (s32[1,512]{1,0:T(1,128)S(1)}, s32[1,512]{1,0:T(1,128)}, u32[]{:S(2)}) copy-start(s32[1,512]{1,0:T(1,128)} %param.13) | copy-start | bytes 6148
  35.5 18.9 %all-to-all-start.1 = ((bf16[128,4,512]{2,1,0:T(4,128)(2,1)}), bf16[128,4,512]{2,1,0:T(4,128)(2,1)}, u32[]{:S(2)}, u32[]{:S(2)}) async-start(bf16[128,4,512]{2,1,0:T(4,128)(2,1)} %reshape.217), calls=%async_computation.1 | async-start | bytes 1048576 | tf_op jit(solution)/shard_map/all_to_all | solution.py:99
  41.2 93.5 %all-gather.2.cloned.1.call-start = ((), (), s32[]{:S(2)}) async-start(), calls=%async_computation.4 | async-start | bytes 8912896 | tf_op jit(solution)/shard_map/all_gather | solution.py:129
  55.6 5.9 %copy-start.6 = (s32[1,512]{1,0:T(1,128)S(1)}, s32[1,512]{1,0:T(1,128)}, u32[]{:S(2)}) copy-start(s32[1,512]{1,0:T(1,128)} %param.14) | copy-start | bytes 6148
  59.7 0.8 copy-start.2
  62.1 11.0 %all-to-all-start.2 = ((s32[16,1,512]{2,1,0:T(1,128)}), s32[16,1,512]{2,1,0:T(1,128)S(1)}, u32[]{:S(2)}, u32[]{:S(2)}) async-start(s32[16,1,512]{2,1,0:T(1,128)} %broadcast_in_dim.52), calls=%async_computation.2 | async-start | bytes 65536 | tf_op jit(solution)/shard_map/all_to_all | solution.py:19
  245.6 19.9 %copy-start.1 = (bf16[512,512]{0,1:T(8,128)(2,1)S(1)}, bf16[512,512]{0,1:T(8,128)(2,1)}, u32[]{:S(2)}) copy-start(bf16[512,512]{0,1:T(8,128)(2,1)} %fusion.32) | copy-start | bytes 1572868
  260.5 15.2 %all-to-all-start.3 = ((bf16[16,2,8192]{2,1,0:T(2,128)(2,1)}), bf16[16,2,8192]{2,1,0:T(2,128)(2,1)S(1)}, u32[]{:S(2)}, u32[]{:S(2)}) async-start(bf16[16,2,8192]{2,1,0:T(2,128)(2,1)} %reshape.239), calls=%async_computation.3 | async-start | bytes 1048576 | tf_op jit(solution)/shard_map/all_to_all | solution.py:135
  284.9 4.0 %copy-start.3 = (bf16[512,512]{0,1:T(8,128)(2,1)S(1)}, bf16[512,512]{0,1:T(8,128)(2,1)}, u32[]{:S(2)}) copy-start(bf16[512,512]{0,1:T(8,128)(2,1)} %copy-done.2) | copy-start | bytes 1572868
  284.9 4.0 %copy-start.4 = (bf16[16,512,1,32]{1,3,0,2:T(8,128)(2,1)S(1)}, bf16[16,512,1,32]{1,3,0,2:T(8,128)(2,1)}, u32[]{:S(2)}) copy-start(bf16[16,512,1,32]{1,3,0,2:T(8,128)(2,1)} %convert_bitcast_fusion) | copy-start | bytes 1572868
Sparse Core Ops, SparseCore 0:
  61.5 73.1 all-gather.1
where the time goes:
time: 306 us; the launch traced here: 305 us
  matrix products  96.7 us (32%)
  waiting for transfers between devices  78 us (25%)
  local copies, waits for them, and re-layouts  61.1 us (20%)
  blocking collectives  20.5 us (7%)
  other arithmetic  14.7 us (5%)
  starting transfers between devices  14.4 us (5%)
  between operations  13.6 us (4%)
  loops' own time  5.8 us (2%)
    dot_general x10, matrix products, add_keys(): jnp.einsum('gqk,kgc->qgc', weights, value_block, preferred_element_type=j...  82.4 us
    all_gather x1, waiting for transfers between devices, local(): lax.all_gather(normed_input, 'seq', axis=0, tiled=True)  61.5 us
    all_to_all x1, blocking collectives, local(): lax.all_to_all(requested, ('emb', 'seq'), split_axis=0, concat_axis=0, ti...  20.5 us
    unnamed x21, local copies, waits for them, and re-layouts  14.4 us
    all_to_all x1, waiting for transfers between devices, local(): lax.all_to_all(cold_table[lax.all_to_all(requested, ('emb', 'seq'), split...  8.09 us
    all_to_all x1, waiting for transfers between devices, local(): lax.all_to_all(attended.reshape(seq_devices, tokens_here * head_groups *...  7.86 us
    gather x2, local copies, waits for them, and re-layouts, local(): cold_table[lax.all_to_all(requested, ('emb', 'seq'), split_axis=0, concat...  7.36 us
    convert_element_type x2, local copies, waits for them, and re-layouts, local(): returned.reshape(seq_devices, tokens_here, head_groups, head_width)  6.41 us
  transfers between devices with their start and end apart: 4, of which 4 were waited for; matrix products, arithmetic and copies ran while one was open for 5% of the time, Pallas kernels for 0%

commit v1 on v0

--- a/solution.py
+++ b/solution.py
@@ -1,3 +1,4 @@
+import functools
 import math
 import jax
 import jax.numpy as jnp
@@ -6,6 +7,19 @@
 
 H = 16
 epsilon = 1e-06
+
+
+def copies_register(array_here, where_dim):
+    return lax.all_to_all(
+        jnp.concatenate(tuple((array_here for _ in range(lax.axis_size("seq")))), axis=where_dim),
+        "seq",
+        where_dim,
+        where_dim,
+        tiled=True,
+    )
+
+
+pass_the_body = functools.partial(copies_register, where_dim=0)
 
 
 def in_order(pieces, dim):
@@ -126,9 +140,7 @@
         :, :, 1:, :
     ].reshape(model_width, head_groups * 3 * head_width)
     gathered = jnp.dot(
-        lax.all_gather(normed_input, "seq", axis=0, tiled=True),
-        own_weight,
-        preferred_element_type=jnp.float32,
+        pass_the_body(normed_input), own_weight, preferred_element_type=jnp.float32
     ).astype(jnp.bfloat16)
     head_rows = gathered.reshape(tokens_here * seq_devices, head_groups, 3, head_width)
     attended = attend(head_rows[:, :, 1], head_rows[:, :, 2], head_rows[:, :, 0], segments)

time: 306 us -> 396 us (1.29)
  waiting for transfers between devices: 78 us -> 143 us
  local copies, waits for them, and re-layouts: 61.1 us -> 84.3 us
  blocking collectives: 20.5 us -> 0 us
  starting transfers between devices: 14.4 us -> 33.6 us
  other arithmetic: 14.7 us -> 31.1 us
  between operations: 13.6 us -> 0.24 us
    all_to_all x0 -> x2, waiting for transfers between devices: none -> 125 us  [the longest x1 117 us: copies_register(): lax.all_to_all(jnp.concatenate(tuple((array_here for _ in range(lax.axis_...]
    all_gather x1 -> x0, waiting for transfers between devices: 61.5 us -> none  [local(): lax.all_gather(normed_input, 'seq', axis=0, tiled=True)]
    all_to_all x1 -> x0, blocking collectives: 20.5 us -> none  [local(): lax.all_to_all(requested, ('emb', 'seq'), split_axis=0, concat_axis=0, ti...]
    all_to_all x0 -> x2, local copies, waits for them, and re-layouts: none -> 19.8 us  [copies_register(): lax.all_to_all(jnp.concatenate(tuple((array_here for _ in range(lax.axis_...]
    all_to_all x0 -> x2, starting transfers between devices: none -> 18.4 us  [the longest x1 11.2 us: local(): lax.all_to_all(requested, ('emb', 'seq'), split_axis=0, concat_axis=0, ti...]
    unnamed x0 -> x15, other arithmetic: none -> 14 us
  transfers between devices with their start and end apart: 4 -> 5, of which waited for: 4 -> 4; matrix products, arithmetic and copies ran while one was open for 5% -> 11% of each run, Pallas kernels for 0% -> 0%
where the time goes in v1:
time: 396 us; the launch traced here: 394 us
  waiting for transfers between devices  143 us (36%)
  matrix products  96.8 us (24%)
  local copies, waits for them, and re-layouts  84.3 us (21%)
  starting transfers between devices  33.6 us (8%)
  other arithmetic  31.1 us (8%)
  loops' own time  5.78 us (1%)
    all_to_all x1, waiting for transfers between devices, copies_register(): lax.all_to_all(jnp.concatenate(tuple((array_here for _ in range(lax.axis_...  117 us
    dot_general x10, matrix products, add_keys(): jnp.einsum('gqk,kgc->qgc', weights, value_block, preferred_element_type=j...  82.4 us
    all_to_all x2, local copies, waits for them, and re-layouts, copies_register(): lax.all_to_all(jnp.concatenate(tuple((array_here for _ in range(lax.axis_...  19.8 us
    unnamed x21, local copies, waits for them, and re-layouts  16.8 us
    unnamed x15, other arithmetic  14 us
    all_to_all x1, starting transfers between devices, local(): lax.all_to_all(requested, ('emb', 'seq'), split_axis=0, concat_axis=0, ti...  11.2 us
    all_to_all x1, waiting for transfers between devices, local(): lax.all_to_all(attended.reshape(seq_devices, tokens_here * head_groups *...  9.79 us
    all_to_all x1, waiting for transfers between devices, local(): lax.all_to_all(requested, ('emb', 'seq'), split_axis=0, concat_axis=0, ti...  8.74 us
  transfers between devices with their start and end apart: 5, of which 4 were waited for; matrix products, arithmetic and copies ran while one was open for 11% of the time, Pallas kernels for 0%

profile of v1, /device:TPU:0, one launch (start us, length us, event | category | flops | bytes accessed | tf_op | source)
XLA Modules:
  0.0 394.4 jit_solution(15225239407448593968)
XLA Ops:
  0.0 1.6 copy.58
  1.6 11.2 %all-to-all-start = ((s32[128,1,4]{2,1,0:T(1,128)}), s32[128,1,4]{2,1,0:T(1,128)S(1)}, u32[]{:S(2)}, u32[]{:S(2)}) async-start(s32[128,1,4]{2,1,0:T(1,128)} %bitcast.9), calls=%async_computation | async-start | bytes 131072 | tf_op jit(solution)/shard_map/all_to_all | solution.py:115
  13.5 8.7 %all-to-all-done = s32[128,1,4]{2,1,0:T(1,128)S(1)} async-done(((s32[128,1,4]{2,1,0:T(1,128)}), s32[128,1,4]{2,1,0:T(1,128)S(1)}, u32[]{:S(2)}, u32[]{:S(2)}) %all-to-all-start) | async-done | bytes 2080 | tf_op jit(solution)/shard_map/all_to_all | solution.py:115
  22.3 6.4 %gather_fusion.1 = bf16[512,512]{1,0:T(8,128)(2,1)S(1)} fusion(bf16[8192,512]{1,0:T(8,128)(2,1)} %param.17, s32[1024]{0:T(1024)S(1)} %get-tuple-element.215), kind=kCustom, calls=%fused_computation.1 | custom fusion | bytes 1050624 | tf_op jit(solution)/shard_map/gather | solution.py:114
  29.7 5.7 %all-to-all-start.1 = ((bf16[128,4,512]{2,1,0:T(4,128)(2,1)}), bf16[128,4,512]{2,1,0:T(4,128)(2,1)}, u32[]{:S(2)}, u32[]{:S(2)}) async-start(bf16[128,4,512]{2,1,0:T(4,128)(2,1)} %reshape.219), calls=%async_computation.1 | async-start | bytes 1048576 | tf_op jit(solution)/shard_map/all_to_all | solution.py:113
  36.2 4.7 %gather_fusion = bf16[512,512]{1,0:T(8,128)(2,1)S(1)} fusion(bf16[4096,512]{1,0:T(8,128)(2,1)} %param.16, s32[1024]{0:T(1024)S(1)} %get-tuple-element.216), kind=kCustom, calls=%fused_computation | custom fusion | bytes 1050624 | tf_op jit(solution)/shard_map/gather | solution.py:125
  41.1 7.5 %all-to-all-done.1 = bf16[128,4,512]{2,1,0:T(4,128)(2,1)} async-done(((bf16[128,4,512]{2,1,0:T(4,128)(2,1)}), bf16[128,4,512]{2,1,0:T(4,128)(2,1)}, u32[]{:S(2)}, u32[]{:S(2)}) %all-to-all-start.1) | async-done | bytes 524320 | tf_op jit(solution)/shard_map/all_to_all | solution.py:113
  49.2 3.5 all-to-all-start.3
  53.9 2.6 gather_fusion.2
  73.0 7.5 %copy.79 = bf16[64,16,8,512]{3,2,0,1:T(8,128)(2,1)} copy(bf16[64,16,8,512]{3,2,1,0:T(8,128)(2,1)} %bitcast.39) | data formatting | bytes 16777216 | tf_op jit(solution)/shard_map/all_to_all | solution.py:13
  80.5 7.2 %all-to-all-start.2 = ((bf16[16,512,512]{1,2,0:T(8,128)(2,1)}), bf16[16,512,512]{1,2,0:T(8,128)(2,1)}, u32[]{:S(2)}, u32[]{:S(2)}) async-start(bf16[16,512,512]{1,2,0:T(8,128)(2,1)} %bitcast.138), calls=%async_computation.2 | async-start | bytes 16777216 | tf_op jit(solution)/shard_map/all_to_all | solution.py:13
  87.8 3.9 %copy.63 = bf16[512,2048]{0,1:T(8,128)(2,1)} copy(bf16[512,2048]{1,0:T(8,128)(2,1)} %param.18) | data formatting | bytes 4194304 | tf_op args[5]
  91.7 1.9 slice.30
  94.7 116.6 %all-to-all-done.2 = bf16[16,512,512]{1,2,0:T(8,128)(2,1)} async-done(((bf16[16,512,512]{1,2,0:T(8,128)(2,1)}), bf16[16,512,512]{1,2,0:T(8,128)(2,1)}, u32[]{:S(2)}, u32[]{:S(2)}) %all-to-all-start.2) | async-done | bytes 8388640 | tf_op jit(solution)/shard_map/all_to_all | solution.py:13
  211.3 12.3 %copy.62 = bf16[16,512,512]{2,1,0:T(8,128)(2,1)} copy(bf16[16,512,512]{1,2,0:T(8,128)(2,1)} %all-to-all-done.2) | data formatting | bytes 16777216 | tf_op jit(solution)/shard_map/all_to_all | solution.py:13
  223.6 6.0 %convolution_convert_fusion = bf16[8192,96]{0,1:T(8,128)(2,1)S(1)} fusion(bf16[8192,512]{1,0:T(8,128)(2,1)} %bitcast.137, bf16[512,96]{0,1:T(8,128)(2,1)S(1)} %bitcast.145), kind=kOutput, calls=%fused_computation.29 | convolution fusion | flops 806092800 | bytes 10059776 | tf_op jit(solution)/shard_map/dot_general | solution.py:142
  231.9 1.3 copy.64
  233.2 2.2 reshape_squeeze.10
  235.5 2.1 copy.65
  237.6 2.2 reshape_squeeze.11
  239.8 2.1 copy.66
  241.9 93.8 %while.25 = (s32[]{:T(128)}, bf16[4,2048,1,32]{1,3,2,0:T(8,128)(2,1)}, s32[4]{0:T(128)S(1)}, bf16[4,2048,1,32]{1,3,2,0:T(8,128)(2,1)S(1)}, s32[4,2048]{1,0:T(4,1...) while((s32[]{:T(128)}, ...), condition=%wide.region_4.5_spmd.clone.clone, body=%wide.region_1.4_spmd.clone.clone.sunk | while | flops 578949120 | bytes 1935356 | solution.py:86
  244.0 8.3 %while.26 = (s32[]{:T(128)}, f32[2048,1,32]{0,2,1:T(8,128)S(1)}, s32[]{:T(128)}, bf16[4,2048,1,32]{1,3,2,0:T(8,128)(2,1)}, s32[2048]{0:T(1024)S(1)}, /*index=5*/...) while((s32[]{:T(128)}, f32[2048,1,32]{0,2,1:T(8,128)S(1)}, ...), condition=%wide.region_3.3_spmd, body=%wide.region_2.2_spmd.sunk | while | flops 578881536 | bytes 984251 | solution.py:81
  244.0 8.2 %fusion.59 = f32[2048,1,32]{0,2,1:T(8,128)S(1)} fusion(f32[2048,1,32]{0,2,1:T(8,128)S(1)} %get-tuple-element.360, s32[2048]{0:T(1024)S(1)} %get-tuple-element.379, s32[2048]{0:T(1024)S(1)} %get-tuple-element.378, s32[2048]{0:T(1024)S(1)} %bitcast.140, s32[2048]{0:T(1024)S(1)} %broadcast_add_fusion.2, ...), kind=kOutput, calls=%fused_computation.13.clone.1 | convolution fusion | flops 578879488 | bytes 951296 | tf_op jit(solution)/shard_map/while/body/eval_jaxpr/while/body/gqk,kgc->qgc/dot_general | solution.py:77
  255.0 16.6 %while.26 = (s32[]{:T(128)}, f32[2048,1,32]{0,2,1:T(8,128)S(1)}, s32[]{:T(128)}, bf16[4,2048,1,32]{1,3,2,0:T(8,128)(2,1)}, s32[2048]{0:T(1024)S(1)}, /*index=5*/...) while((s32[]{:T(128)}, f32[2048,1,32]{0,2,1:T(8,128)S(1)}, ...), condition=%wide.region_3.3_spmd, body=%wide.region_2.2_spmd.sunk | while | flops 578881536 | bytes 984251 | solution.py:81
  255.0 8.2 %fusion.59 = f32[2048,1,32]{0,2,1:T(8,128)S(1)} fusion(f32[2048,1,32]{0,2,1:T(8,128)S(1)} %get-tuple-element.360, s32[2048]{0:T(1024)S(1)} %get-tuple-element.379, s32[2048]{0:T(1024)S(1)} %get-tuple-element.378, s32[2048]{0:T(1024)S(1)} %bitcast.140, s32[2048]{0:T(1024)S(1)} %broadcast_add_fusion.2, ...), kind=kOutput, calls=%fused_computation.13.clone.1 | convolution fusion | flops 578879488 | bytes 951296 | tf_op jit(solution)/shard_map/while/body/eval_jaxpr/while/body/gqk,kgc->qgc/dot_general | solution.py:77
  263.3 8.2 %fusion.59 = f32[2048,1,32]{0,2,1:T(8,128)S(1)} fusion(f32[2048,1,32]{0,2,1:T(8,128)S(1)} %get-tuple-element.360, s32[2048]{0:T(1024)S(1)} %get-tuple-element.379, s32[2048]{0:T(1024)S(1)} %get-tuple-element.378, s32[2048]{0:T(1024)S(1)} %bitcast.140, s32[2048]{0:T(1024)S(1)} %broadcast_add_fusion.2, ...), kind=kOutput, calls=%fused_computation.13.clone.1 | convolution fusion | flops 578879488 | bytes 951296 | tf_op jit(solution)/shard_map/while/body/eval_jaxpr/while/body/gqk,kgc->qgc/dot_general | solution.py:77
  274.3 24.9 %while.26 = (s32[]{:T(128)}, f32[2048,1,32]{0,2,1:T(8,128)S(1)}, s32[]{:T(128)}, bf16[4,2048,1,32]{1,3,2,0:T(8,128)(2,1)}, s32[2048]{0:T(1024)S(1)}, /*index=5*/...) while((s32[]{:T(128)}, f32[2048,1,32]{0,2,1:T(8,128)S(1)}, ...), condition=%wide.region_3.3_spmd, body=%wide.region_2.2_spmd.sunk | while | flops 578881536 | bytes 984251 | solution.py:81
  274.3 8.2 %fusion.59 = f32[2048,1,32]{0,2,1:T(8,128)S(1)} fusion(f32[2048,1,32]{0,2,1:T(8,128)S(1)} %get-tuple-element.360, s32[2048]{0:T(1024)S(1)} %get-tuple-element.379, s32[2048]{0:T(1024)S(1)} %get-tuple-element.378, s32[2048]{0:T(1024)S(1)} %bitcast.140, s32[2048]{0:T(1024)S(1)} %broadcast_add_fusion.2, ...), kind=kOutput, calls=%fused_computation.13.clone.1 | convolution fusion | flops 578879488 | bytes 951296 | tf_op jit(solution)/shard_map/while/body/eval_jaxpr/while/body/gqk,kgc->qgc/dot_general | solution.py:77
  282.6 8.2 %fusion.59 = f32[2048,1,32]{0,2,1:T(8,128)S(1)} fusion(f32[2048,1,32]{0,2,1:T(8,128)S(1)} %get-tuple-element.360, s32[2048]{0:T(1024)S(1)} %get-tuple-element.379, s32[2048]{0:T(1024)S(1)} %get-tuple-element.378, s32[2048]{0:T(1024)S(1)} %bitcast.140, s32[2048]{0:T(1024)S(1)} %broadcast_add_fusion.2, ...), kind=kOutput, calls=%fused_computation.13.clone.1 | convolution fusion | flops 578879488 | bytes 951296 | tf_op jit(solution)/shard_map/while/body/eval_jaxpr/while/body/gqk,kgc->qgc/dot_general | solution.py:77
  290.9 8.2 %fusion.59 = f32[2048,1,32]{0,2,1:T(8,128)S(1)} fusion(f32[2048,1,32]{0,2,1:T(8,128)S(1)} %get-tuple-element.360, s32[2048]{0:T(1024)S(1)} %get-tuple-element.379, s32[2048]{0:T(1024)S(1)} %get-tuple-element.378, s32[2048]{0:T(1024)S(1)} %bitcast.140, s32[2048]{0:T(1024)S(1)} %broadcast_add_fusion.2, ...), kind=kOutput, calls=%fused_computation.13.clone.1 | convolution fusion | flops 578879488 | bytes 951296 | tf_op jit(solution)/shard_map/while/body/eval_jaxpr/while/body/gqk,kgc->qgc/dot_general | solution.py:77
  301.9 33.2 %while.26 = (s32[]{:T(128)}, f32[2048,1,32]{0,2,1:T(8,128)S(1)}, s32[]{:T(128)}, bf16[4,2048,1,32]{1,3,2,0:T(8,128)(2,1)}, s32[2048]{0:T(1024)S(1)}, /*index=5*/...) while((s32[]{:T(128)}, f32[2048,1,32]{0,2,1:T(8,128)S(1)}, ...), condition=%wide.region_3.3_spmd, body=%wide.region_2.2_spmd.sunk | while | flops 578881536 | bytes 984251 | solution.py:81
  301.9 8.2 %fusion.59 = f32[2048,1,32]{0,2,1:T(8,128)S(1)} fusion(f32[2048,1,32]{0,2,1:T(8,128)S(1)} %get-tuple-element.360, s32[2048]{0:T(1024)S(1)} %get-tuple-element.379, s32[2048]{0:T(1024)S(1)} %get-tuple-element.378, s32[2048]{0:T(1024)S(1)} %bitcast.140, s32[2048]{0:T(1024)S(1)} %broadcast_add_fusion.2, ...), kind=kOutput, calls=%fused_computation.13.clone.1 | convolution fusion | flops 578879488 | bytes 951296 | tf_op jit(solution)/shard_map/while/body/eval_jaxpr/while/body/gqk,kgc->qgc/dot_general | solution.py:77
  310.2 8.2 %fusion.59 = f32[2048,1,32]{0,2,1:T(8,128)S(1)} fusion(f32[2048,1,32]{0,2,1:T(8,128)S(1)} %get-tuple-element.360, s32[2048]{0:T(1024)S(1)} %get-tuple-element.379, s32[2048]{0:T(1024)S(1)} %get-tuple-element.378, s32[2048]{0:T(1024)S(1)} %bitcast.140, s32[2048]{0:T(1024)S(1)} %broadcast_add_fusion.2, ...), kind=kOutput, calls=%fused_computation.13.clone.1 | convolution fusion | flops 578879488 | bytes 951296 | tf_op jit(solution)/shard_map/while/body/eval_jaxpr/while/body/gqk,kgc->qgc/dot_general | solution.py:77
  318.5 8.2 %fusion.59 = f32[2048,1,32]{0,2,1:T(8,128)S(1)} fusion(f32[2048,1,32]{0,2,1:T(8,128)S(1)} %get-tuple-element.360, s32[2048]{0:T(1024)S(1)} %get-tuple-element.379, s32[2048]{0:T(1024)S(1)} %get-tuple-element.378, s32[2048]{0:T(1024)S(1)} %bitcast.140, s32[2048]{0:T(1024)S(1)} %broadcast_add_fusion.2, ...), kind=kOutput, calls=%fused_computation.13.clone.1 | convolution fusion | flops 578879488 | bytes 951296 | tf_op jit(solution)/shard_map/while/body/eval_jaxpr/while/body/gqk,kgc->qgc/dot_general | solution.py:77
  326.8 8.2 %fusion.59 = f32[2048,1,32]{0,2,1:T(8,128)S(1)} fusion(f32[2048,1,32]{0,2,1:T(8,128)S(1)} %get-tuple-element.360, s32[2048]{0:T(1024)S(1)} %get-tuple-element.379, s32[2048]{0:T(1024)S(1)} %get-tuple-element.378, s32[2048]{0:T(1024)S(1)} %bitcast.140, s32[2048]{0:T(1024)S(1)} %broadcast_add_fusion.2, ...), kind=kOutput, calls=%fused_computation.13.clone.1 | convolution fusion | flops 578879488 | bytes 951296 | tf_op jit(solution)/shard_map/while/body/eval_jaxpr/while/body/gqk,kgc->qgc/dot_general | solution.py:77
  335.8 2.8 copy.67
  338.6 5.4 %all_to_all.38 = bf16[16,1,16384]{2,1,0:T(2,128)(2,1)} reshape(bf16[4,2048,1,32]{3,1,0,2:T(8,128)(2,1)} %copy.67) | data formatting | bytes 1048576 | tf_op jit(solution)/shard_map/all_to_all | solution.py:147
  344.5 5.7 %reduce.9 = bf16[16,16384]{1,0:T(8,128)(2,1)} reduce(bf16[16,1,16384]{2,1,0:T(2,128)(2,1)} %all_to_all.38, bf16[]{:T(256)} %broadcast.198), dimensions={1}, to_apply=%all_to_all.38.reduce_sub_computation | reduce | bytes 1048578 | tf_op jit(solution)/shard_map/all_to_all | solution.py:147
  350.2 2.2 reshape.241
  352.4 6.0 %all-to-all-start.4 = ((bf16[16,2,8192]{2,1,0:T(2,128)(2,1)}), bf16[16,2,8192]{2,1,0:T(2,128)(2,1)}, u32[]{:S(2)}, u32[]{:S(2)}) async-start(bf16[16,2,8192]{2,1,0:T(2,128)(2,1)} %reshape.241), calls=%async_computation.4 | async-start | bytes 1048576 | tf_op jit(solution)/shard_map/all_to_all | solution.py:147
  358.9 9.8 %all-to-all-done.4 = bf16[16,2,8192]{2,1,0:T(2,128)(2,1)} async-done(((bf16[16,2,8192]{2,1,0:T(2,128)(2,1)}), bf16[16,2,8192]{2,1,0:T(2,128)(2,1)}, u32[]{:S(2)}, u32[]{:S(2)}) %all-to-all-start.4) | async-done | bytes 524320 | tf_op jit(solution)/shard_map/all_to_all | solution.py:147
  368.7 3.5 reshape.242
  372.2 5.6 %fusion.33 = (f32[16384]{0:T(1024)S(1)}, f32[16,16384]{1,0:T(8,128)}) fusion(bf16[16,1,16384]{2,1,0:T(2,128)(2,1)} %reshape.242), kind=kLoop, calls=%fused_computation.50 | loop fusion | flops 770048 | bytes 1638400 | tf_op jit(solution)/shard_map/reduce_sum | solution.py:157
  377.8 3.7 reshape.209
  381.6 3.6 copy.69
  385.5 3.0 multiply_reduce_fusion
  388.5 5.0 %fusion.26 = bf16[1,512,512]{1,2,0:T(8,128)(2,1)S(1)} fusion(f32[512,512]{0,1:T(8,128)} %get-tuple-element.214, bf16[2048,512]{1,0:T(8,128)(2,1)S(1)} %copy-done, bf16[512,2048]{1,0:T(8,128)(2,1)} %param.20, f32[512]{0:T(512)S(1)} %add_rsqrt_fusion), kind=kOutput, calls=%fused_computation.41 | convolution fusion | flops 2153775104 | bytes 5769216 | tf_op jit(solution)/shard_map/dot_general | solution.py:172
  (108 shorter events, 32.2 us)
Async XLA Ops:
  0.0 388.5 %copy-start = (bf16[2048,512]{1,0:T(8,128)(2,1)S(1)}, bf16[2048,512]{1,0:T(8,128)(2,1)}, u32[]{:S(2)}) copy-start(bf16[2048,512]{1,0:T(8,128)(2,1)} %param.21) | copy-start | bytes 6291460
  0.0 48.6 %copy-start.6 = (s32[1,512]{1,0:T(1,128)S(1)}, s32[1,512]{1,0:T(1,128)}, u32[]{:S(2)}) copy-start(s32[1,512]{1,0:T(1,128)} %param.14) | copy-start | bytes 6148
  1.6 20.6 %all-to-all-start = ((s32[128,1,4]{2,1,0:T(1,128)}), s32[128,1,4]{2,1,0:T(1,128)S(1)}, u32[]{:S(2)}, u32[]{:S(2)}) async-start(s32[128,1,4]{2,1,0:T(1,128)} %bitcast.9), calls=%async_computation | async-start | bytes 131072 | tf_op jit(solution)/shard_map/all_to_all | solution.py:115
  29.7 18.9 %all-to-all-start.1 = ((bf16[128,4,512]{2,1,0:T(4,128)(2,1)}), bf16[128,4,512]{2,1,0:T(4,128)(2,1)}, u32[]{:S(2)}, u32[]{:S(2)}) async-start(bf16[128,4,512]{2,1,0:T(4,128)(2,1)} %reshape.219), calls=%async_computation.1 | async-start | bytes 1048576 | tf_op jit(solution)/shard_map/all_to_all | solution.py:113
  49.2 31.3 %all-to-all-start.3 = ((s32[16,1,512]{2,1,0:T(1,128)}), s32[16,1,512]{2,1,0:T(1,128)S(1)}, u32[]{:S(2)}, u32[]{:S(2)}) async-start(s32[16,1,512]{2,1,0:T(1,128)} %broadcast_in_dim.52), calls=%async_computation.3 | async-start | bytes 65536 | tf_op jit(solution)/shard_map/all_to_all | solution.py:33
  58.0 15.0 %copy-start.1 = (bf16[512,512]{0,1:T(8,128)(2,1)}, bf16[512,512]{0,1:T(8,128)(2,1)S(1)}, u32[]{:S(2)}) copy-start(bf16[512,512]{0,1:T(8,128)(2,1)S(1)} %get-tuple-element.207) | copy-start | bytes 1572868
  58.0 15.0 %copy-start.4 = (f32[512]{0:T(512)}, f32[512]{0:T(512)S(1)}, u32[]{:S(2)}) copy-start(f32[512]{0:T(512)S(1)} %add_rsqrt_fusion.2) | copy-start | bytes 6148
  80.5 130.7 %all-to-all-start.2 = ((bf16[16,512,512]{1,2,0:T(8,128)(2,1)}), bf16[16,512,512]{1,2,0:T(8,128)(2,1)}, u32[]{:S(2)}, u32[]{:S(2)}) async-start(bf16[16,512,512]{1,2,0:T(8,128)(2,1)} %bitcast.138), calls=%async_computation.2 | async-start | bytes 16777216 | tf_op jit(solution)/shard_map/all_to_all | solution.py:13
  335.8 22.6 %copy-start.2 = (bf16[512,512]{0,1:T(8,128)(2,1)S(1)}, bf16[512,512]{0,1:T(8,128)(2,1)}, u32[]{:S(2)}) copy-start(bf16[512,512]{0,1:T(8,128)(2,1)} %copy-done.1) | copy-start | bytes 1572868
  335.8 22.6 %copy-start.3 = (bf16[512,16,1,1,32]{0,4,3,1,2:T(8,128)(2,1)S(1)}, bf16[512,16,1,1,32]{0,4,3,1,2:T(8,128)(2,1)}, u32[]{:S(2)}) copy-start(bf16[512,16,1,1,32]{0,4,3,1,2:T(8,128)(2,1)} %slice.30) | copy-start | bytes 1572868
  335.8 22.6 %copy-start.5 = (f32[512]{0:T(512)S(1)}, f32[512]{0:T(512)}, u32[]{:S(2)}) copy-start(f32[512]{0:T(512)} %copy-done.4) | copy-start | bytes 6148
  352.4 16.3 %all-to-all-start.4 = ((bf16[16,2,8192]{2,1,0:T(2,128)(2,1)}), bf16[16,2,8192]{2,1,0:T(2,128)(2,1)}, u32[]{:S(2)}, u32[]{:S(2)}) async-start(bf16[16,2,8192]{2,1,0:T(2,128)(2,1)} %reshape.241), calls=%async_computation.4 | async-start | bytes 1048576 | tf_op jit(solution)/shard_map/all_to_all | solution.py:147
